TPU v7x, 32 devices: a whole 2x2x4 slice. The times are simulated.
32 devices in a mesh: tm: 4 (over x, core), batch: 8 (over z, y).
Axes of the slice: x: 2, y: 2, z: 4, core: 2. Of those that a mesh axis runs over, the one named last changes fastest.
Arguments:
- latents: float32 [8, 16, 4096], P('tm', None, 'batch'), may hold values from -6 to 6
- shifts: int32 [16], replicated, may hold values from 0 to 7
- starts: int32 [16], replicated, may hold values from 0 to 2
- labels: int32 [16], replicated, may hold values from 0 to 1000
- class_table: bfloat16 [1001, 1152], replicated, may hold values from -6 to 6
- w_freq: bfloat16 [256, 1152], replicated, may hold values from -0.375 to 0.375
- w_time: bfloat16 [1152, 1152], replicated, may hold values from -0.1875 to 0.1875
- w_ada: bfloat16 [1152, 9216], P(None, 'tm'), may hold values from -0.1875 to 0.1875
- w_patch: bfloat16 [16, 1152], replicated, may hold values from -1.5 to 1.5
- w_qkv: bfloat16 [1152, 3456], P('batch', 'tm'), may hold values from -1 to 1
- w_proj: bfloat16 [1152, 1152], P('tm', 'batch'), may hold values from -0.1875 to 0.1875
- w_fc1: bfloat16 [1152, 4608], P('batch', 'tm'), may hold values from -0.1875 to 0.1875
- w_fc2: bfloat16 [4608, 1152], P('tm', 'batch'), may hold values from -0.09375 to 0.09375
- w_final: bfloat16 [1152, 16], replicated, may hold values from -0.1875 to 0.1875
Outputs:
- new_latents: float32 [8, 16, 4096], P('tm', None, 'batch')
- velocity: bfloat16 [8, 16, 4096], P('tm', None, 'batch')
All inputs are finite; a program needn't handle non-finite values.
Results may differ from a plain program's by a relative error of at most 0.0091.
Values may be sent and summed in bfloat16 or wider, within the bound.
A program may use at most 128 MiB of HBM per device.

v0:
```python
import functools
import math

import jax
import jax.numpy as jnp
import numpy as np
from jax import lax
from jax.experimental import pallas as pl
from jax.experimental.pallas import tpu as pltpu
from jax.sharding import PartitionSpec as P

D = 1152
HEADS = 16
FREQ = 256
GRID = 16
STEPS = 18
LANES = 128
CORES = 2
MESH = pl.DeviceIdType.MESH


def entering(part, axis, combine, identity):
    place = lax.axis_index(axis)
    gathered = lax.all_gather(part, axis)
    state = jnp.zeros_like(part) + jnp.asarray(identity, part.dtype)

    def one(lap, state):
        return combine(state, lax.dynamic_index_in_dim(gathered, lap, 0, False))

    return lax.fori_loop(0, place, one, state)


def layer_norm(values):
    average = jnp.mean(values, axis=-1, keepdims=True)
    centred = values - average
    variance = jnp.mean(centred * centred, axis=-1, keepdims=True)
    return centred * lax.rsqrt(variance + 1e-06)


def position_table(token_count, group):
    token_ids = np.arange(token_count).reshape(token_count // group, group).T.reshape(-1)
    row_ids = (token_ids // GRID).astype(np.float32)
    col_ids = (token_ids % GRID).astype(np.float32)
    quarter = D // 4
    omegas = np.exp(-math.log(10000.0) * np.arange(quarter, dtype=np.float32) / quarter).astype(np.float32)
    col_angle = col_ids[:, None] * omegas[None, :]
    row_angle = row_ids[:, None] * omegas[None, :]
    return np.concatenate(
        [np.sin(col_angle), np.cos(col_angle), np.sin(row_angle), np.cos(row_angle)], axis=1
    ).astype(np.float32)

def cond_activation(step_ids, class_ids, class_table, w_freq, w_time):
    half_freq = FREQ // 2
    freqs = jnp.exp(-math.log(10000.0) * jnp.arange(half_freq, dtype=jnp.float32) / half_freq)
    tvalue = 1000.0 * (1.0 - step_ids.astype(jnp.float32) / STEPS)
    angles = tvalue[:, None] * freqs[None, :]
    embedded = jnp.concatenate([jnp.cos(angles), jnp.sin(angles)], axis=1).astype(jnp.bfloat16)
    hidden_time = jax.nn.silu(jnp.dot(embedded, w_freq, preferred_element_type=jnp.float32)).astype(
        jnp.bfloat16
    )
    condition = jnp.dot(hidden_time, w_time, preferred_element_type=jnp.float32) + jnp.take(
        class_table, class_ids, axis=0
    ).astype(jnp.float32)
    return jax.nn.silu(condition).astype(jnp.bfloat16)


def times_transposed(left, right):
    return lax.dot_general(
        left, right, (((1,), (1,)), ((), ())), preferred_element_type=jnp.float32
    )


def attention_product(rows_in, entry, head_count, head_size):
    qkv_width = 3 * head_count * head_size
    boundary = qkv_width // LANES * LANES
    rows = jnp.dot(rows_in, entry[:, :qkv_width], preferred_element_type=jnp.float32)
    rows = rows.astype(jnp.bfloat16)
    scale = 1.0 / math.sqrt(head_size)
    pieces = []
    if qkv_width > boundary:
        pieces.append(jnp.zeros((rows.shape[0], qkv_width - boundary), jnp.bfloat16))
    for head in range(head_count):
        start = head * 3 * head_size
        query = rows[:, start : start + head_size]
        keys = rows[:, start + head_size : start + 2 * head_size]
        values = rows[:, start + 2 * head_size : start + 3 * head_size]
        scores = times_transposed(query, keys)
        peak = jnp.max(scores, axis=-1, keepdims=True)
        weights = jnp.exp((scores - peak) * scale)
        total = jnp.sum(weights, axis=-1, keepdims=True)
        mixed = jnp.dot(
            weights.astype(jnp.bfloat16), values, preferred_element_type=jnp.float32
        )
        pieces.append((mixed / total).astype(jnp.bfloat16))
    attended = jnp.concatenate(pieces, axis=1)
    return times_transposed(attended, entry[:, boundary:])


class Gather:
    def __init__(self, sizes, own, buf, send_sem, z_sem, x_sem, y_sem, d_sem, p_sem):
        self.xs, self.ys, self.zs = sizes
        self.own, self.buf = own, buf
        self.send_sem, self.z_sem, self.x_sem = send_sem, z_sem, x_sem
        self.y_sem, self.d_sem, self.p_sem = y_sem, d_sem, p_sem
        tm, batch = lax.axis_index("tm"), lax.axis_index("batch")
        self.x, self.c = tm // CORES, tm % CORES
        self.z, self.y = batch // self.ys, batch % self.ys
        self.tm, self.batch = tm, batch
        rows = own.shape[1]
        self.cut = (rows // 32) * 16
        self.whole = pl.ds(0, rows)
        self.first = pl.ds(0, rows - self.cut)
        self.last = pl.ds(rows - self.cut, self.cut)

    def peer(self, position, step, size):
        return (position + step) % size

    def along_z(self, step):
        direction = 1 - 2 * (self.z * 2 // self.zs)
        return (self.z + direction * step + self.zs) % self.zs

    def device(self, x, c, z, y):
        return {"tm": x * CORES + c, "batch": z * self.ys + y}

    def peers(self):
        out = [self.device(self.x, 1 - self.c, self.z, self.y)]
        for step in range(1, self.zs):
            out.append(self.device(self.x, self.c, self.along_z(step), self.y))
        for step in range(1, self.xs):
            out.append(self.device(self.peer(self.x, step, self.xs), self.c, self.z, self.y))
        for step in range(1, self.ys):
            out.append(self.device(self.x, self.c, self.z, self.peer(self.y, step, self.ys)))
        return out

    def greet(self):
        barrier = pltpu.get_barrier_semaphore()
        for device in self.peers():
            pl.semaphore_signal(barrier, inc=1, device_id=device, device_id_type=MESH)

    def met(self):
        pl.semaphore_wait(pltpu.get_barrier_semaphore(), len(self.peers()))

    def place(self, k, x, z, y, rows):
        return self.buf.at[k, x * CORES + self.c, z * self.ys + y, rows]

    def send(self, k, kind, block, rows, device, arrival, own=False):
        target = self.place(k, *block, rows)
        source = self.own.at[k, rows] if own else target
        pltpu.make_async_remote_copy(
            src_ref=source,
            dst_ref=target,
            send_sem=self.send_sem.at[k, kind],
            recv_sem=arrival,
            device_id=device,
            device_id_type=MESH,
        ).start()

    def arrived(self, k, block, arrival):
        region = self.place(k, *block, self.whole)
        pltpu.make_async_copy(region, region, arrival).wait()

    def to_partner(self, k, block, own=False):
        device = self.device(self.x, 1 - self.c, self.z, self.y)
        self.send(k, 0, block, self.whole, device, self.p_sem.at[k, block[0]], own)

    def to_z(self, k):
        block = (self.x, self.z, self.y)
        for step in range(1, self.zs):
            device = self.device(self.x, self.c, self.along_z(step), self.y)
            self.send(k, 1, block, self.whole, device, self.z_sem.at[k, self.z], True)

    def to_x(self, k, block, own=False):
        for step in range(1, self.xs):
            device = self.device(self.peer(self.x, step, self.xs), self.c, self.z, self.y)
            arrival = self.x_sem.at[k, block[1] * self.xs + self.x]
            self.send(k, 2, block, self.whole, device, arrival, own)

    def to_y(self, k, block, own=False):
        for step in range(1, self.ys):
            device = self.device(self.x, self.c, self.z, self.peer(self.y, step, self.ys))
            arrival = self.y_sem.at[k, block[1] * self.ys + self.y]
            self.send(k, 3, block, self.whole, device, arrival, own)

    def own_out(self, k):
        block = (self.x, self.z, self.y)
        self.to_y(k, block, True)
        self.to_x(k, block, True)
        self.to_partner(k, block, True)

    def from_z(self, k, step):
        z = self.along_z(step)
        block = (self.x, z, self.y)
        self.arrived(k, block, self.z_sem.at[k, z])
        self.to_y(k, block)
        self.to_x(k, block)
        self.to_partner(k, block)

    def from_xy(self, k, step):
        z = self.along_z(step)
        for ystep in range(1, self.ys):
            y = self.peer(self.y, ystep, self.ys)
            block = (self.x, z, y)
            self.arrived(k, block, self.y_sem.at[k, z * self.ys + y])
            for step in range(1, self.xs):
                device = self.device(self.peer(self.x, step, self.xs), self.c, self.z, self.y)
                self.send(k, 4, block, self.first, device, self.d_sem.at[k, self.x])
            self.to_partner(k, block)
        for xstep in range(1, self.xs):
            x = self.peer(self.x, xstep, self.xs)
            block = (x, z, self.y)
            self.arrived(k, block, self.x_sem.at[k, z * self.xs + x])
            for step in range(1, self.ys):
                device = self.device(self.x, self.c, self.z, self.peer(self.y, step, self.ys))
                self.send(k, 4, block, self.last, device, self.d_sem.at[k, x])
            self.to_partner(k, block)

    def from_diagonal(self, k):
        count = self.zs * (self.ys - 1)
        for xstep in range(1, self.xs):
            x = self.peer(self.x, xstep, self.xs)
            if count:
                region = self.buf.at[k, 0, pl.ds(0, count)]
                pltpu.make_async_copy(region, region, self.d_sem.at[k, x]).wait()
            for ystep in range(1, self.ys):
                for z in range(self.zs):
                    self.to_partner(k, (x, z, self.peer(self.y, ystep, self.ys)))

    def from_partner(self, k, x):
        region = self.buf.at[k, 0]
        pltpu.make_async_copy(region, region, self.p_sem.at[k, x]).wait()

    def all_left(self, k):
        xs, ys, zs = self.xs, self.ys, self.zs
        regions = [self.buf.at[k, pl.ds(0, xs)]]
        regions.append(self.buf.at[k, 0, pl.ds(0, zs - 1)] if zs > 1 else None)
        regions.append(self.buf.at[k, pl.ds(0, xs - 1), pl.ds(0, zs)] if xs > 1 else None)
        regions.append(self.buf.at[k, 0, pl.ds(0, zs * (ys - 1))] if ys > 1 else None)
        both = xs > 1 and ys > 1
        regions.append(self.buf.at[k, pl.ds(0, xs - 1), pl.ds(0, zs * (ys - 1))] if both else None)
        for kind, region in enumerate(regions):
            if region is not None:
                pltpu.make_async_copy(region, region, self.send_sem.at[k, kind]).wait()


def denoise_kernel(
    sizes, head_count, head_size,
    patch_ref, mod_ref, w_patch_ref, w_final_ref, pos_ref, own_ref, out_ref,
    buf, tokens, normed, hidden, send_sem, z_sem, x_sem, y_sem, d_sem, p_sem,
):
    points, lane_rows, lanes = patch_ref.shape
    patch_size, width = w_patch_ref.shape
    group = lanes // patch_size
    token_count = lane_rows * group
    shards = sizes[0] * CORES
    block_rows, block_width = own_ref.shape[1:]
    gather = Gather(sizes, own_ref, buf, send_sem, z_sem, x_sem, y_sem, d_sem, p_sem)
    gather.greet()
    for k in range(3):
        buf[k, gather.tm, gather.batch] = own_ref[k]
    gather.met()
    gather.own_out(0)
    for k in range(3):
        gather.to_z(k)

    def part(point, index):
        return mod_ref[point, pl.ds(index, 1), :]

    def modulated(values, point, index):
        return (layer_norm(values) * (1.0 + part(point, index + 1)) + part(point, index)).astype(
            jnp.bfloat16
        )

    def enter(point, carry):
        flat = patch_ref[point]
        pieces = [flat[:, k * patch_size : (k + 1) * patch_size] for k in range(group)]
        value = jnp.dot(
            jnp.concatenate(pieces, axis=0), w_patch_ref[...], preferred_element_type=jnp.float32
        )
        value = value + pos_ref[...]
        tokens[point] = value
        normed[point] = modulated(value, point, 0)
        return carry

    lax.fori_loop(0, points, enter, 0)

    for step in range(sizes[2]):
        if step:
            gather.from_z(0, step)
        if step > 1:
            gather.from_xy(0, step - 2)
    gather.from_xy(0, max(sizes[2] - 2, 0))
    if sizes[2] > 1:
        gather.from_xy(0, sizes[2] - 1)
    gather.own_out(1)

    def weights(k, shard):
        return buf[k, shard].reshape(sizes[1] * sizes[2] * block_rows, block_width)

    def shard_of(turn):
        x = (gather.x + turn // CORES) % sizes[0]
        return x, x * CORES + (gather.c + turn % CORES) % CORES

    total_steps = shards * points

    def sweep(k, events, body):
        at = {}
        for share, event in events:
            at.setdefault(int(share * total_steps), []).append(event)

        def one(step, carry):
            turn, point = step // points, step % points
            x, shard = shard_of(turn)
            for when, todo in at.items():
                @pl.when(step == when)
                def _():
                    for event in todo:
                        event()

            @pl.when((point == 0) & (turn % CORES == 1))
            def _():
                gather.from_partner(k, x)

            body(shard, point)
            return carry

        lax.fori_loop(0, total_steps, one, 0)

    def relay(k, start, stop, last):
        todo = []
        zs = sizes[2]
        for step in range(1, zs):
            todo.append(functools.partial(gather.from_z, k, step))
            if step > 1:
                todo.append(functools.partial(gather.from_xy, k, step - 2))
        for step in range(max(zs - 2, 0), zs):
            todo.append(functools.partial(gather.from_xy, k, step))
        if last is not None:
            todo.append(functools.partial(gather.own_out, last))
        count = len(todo)
        return [(start + (stop - start) * i / max(count - 1, 1), e) for i, e in enumerate(todo)]

    def attention_step(shard, point):
        product = attention_product(normed[point], weights(0, shard), head_count, head_size)
        tokens[point] += part(point, 2) * product

    half = CORES / shards
    sweep(
        0,
        [(half, functools.partial(gather.from_diagonal, 0))] + relay(1, 0.1, 0.8, 2),
        attention_step,
    )

    def second(point, carry):
        normed[point] = modulated(tokens[point], point, 3)
        return carry

    lax.fori_loop(0, points, second, 0)

    def hidden_step(shard, point):
        value = jnp.dot(normed[point], weights(1, shard), preferred_element_type=jnp.float32)
        hidden[shard, point] = jax.nn.gelu(value, approximate=True).astype(jnp.bfloat16)

    sweep(
        1,
        [(half, functools.partial(gather.from_diagonal, 1))] + relay(2, 0.0, 0.95, None),
        hidden_step,
    )

    def residual_step(shard, point):
        product = times_transposed(hidden[shard, point], weights(2, shard))
        tokens[point] += part(point, 5) * product

    sweep(2, [(half, functools.partial(gather.from_diagonal, 2))], residual_step)

    def leave(point, carry):
        final_in = modulated(tokens[point], point, 6)
        value = jnp.dot(final_in, w_final_ref[...], preferred_element_type=jnp.float32)
        pieces = [value[k * lane_rows : (k + 1) * lane_rows, :] for k in range(group)]
        out_ref[point] = jnp.concatenate(pieces, axis=1).astype(jnp.bfloat16)
        return carry

    lax.fori_loop(0, points, leave, 0)
    for k in range(3):
        gather.all_left(k)


def denoise(patch_rows, modulation, w_patch, w_final, own, sizes):
    points, lane_rows, lanes = patch_rows.shape
    patch_size, width = w_patch.shape
    group = lanes // patch_size
    token_count = lane_rows * group
    xs, ys, zs = sizes
    shards, blocks = xs * CORES, ys * zs
    block_rows, block_width = own.shape[1:]
    pos = jnp.asarray(position_table(token_count, group))
    dma = pltpu.SemaphoreType.DMA
    head_size = width // HEADS
    vmem = pl.BlockSpec(memory_space=pltpu.VMEM)
    return pl.pallas_call(
        functools.partial(denoise_kernel, sizes, HEADS // shards, head_size),
        out_shape=jax.ShapeDtypeStruct(patch_rows.shape, jnp.bfloat16),
        in_specs=[vmem] * 6,
        out_specs=vmem,
        scratch_shapes=[
            pltpu.VMEM((3, shards, blocks, block_rows, block_width), jnp.bfloat16),
            pltpu.VMEM((points, token_count, width), jnp.float32),
            pltpu.VMEM((points, token_count, width), jnp.bfloat16),
            pltpu.VMEM((shards, points, token_count, block_width), jnp.bfloat16),
            dma((3, 5)),
            dma((3, zs)),
            dma((3, zs * xs)),
            dma((3, zs * ys)),
            dma((3, xs)),
            dma((3, xs)),
        ],
        compiler_params=pltpu.CompilerParams(
            collective_id=0, has_side_effects=True, vmem_limit_bytes=66_000_000
        ),
        name="denoise",
    )(patch_rows, modulation, w_patch, w_final, pos, own)


def add_pair(earlier, later):
    return earlier + later


def local(
    sizes,
    latents,
    shifts,
    starts,
    labels,
    class_table,
    w_freq,
    w_time,
    w_ada,
    w_patch,
    w_qkv,
    w_proj,
    w_fc1,
    w_fc2,
    w_final,
):
    tm_count = lax.axis_size("tm")
    tm_index = lax.axis_index("tm")
    batch_index = lax.axis_index("batch")
    local_steps = latents.shape[0]
    window = local_steps * tm_count
    sample_total, lat_block = latents.shape[1:]
    lane_rows = lat_block // LANES
    whole = lax.all_gather(latents, "tm", axis=0, tiled=True)
    local_positions = tm_index * local_steps + jnp.arange(local_steps, dtype=jnp.int32)[:, None]
    source_rows = jnp.minimum(local_positions + shifts[None, :], window - 1)
    points = jnp.take_along_axis(whole, source_rows[:, :, None], axis=0)
    anchor = jnp.take_along_axis(whole, shifts[None, :, None], axis=0)[0]
    by_sample = lax.all_to_all(
        points.astype(jnp.bfloat16).reshape(local_steps, sample_total, lane_rows, LANES),
        "batch",
        split_axis=1,
        concat_axis=2,
        tiled=True,
    )
    sample_count = by_sample.shape[1]
    own_shifts = lax.dynamic_slice_in_dim(shifts, batch_index * sample_count, sample_count)
    own_starts = lax.dynamic_slice_in_dim(starts, batch_index * sample_count, sample_count)
    own_labels = lax.dynamic_slice_in_dim(labels, batch_index * sample_count, sample_count)
    window_positions = jnp.arange(window, dtype=jnp.int32)[:, None]
    step_ids = (own_starts + own_shifts)[None, :] + window_positions
    class_ids = jnp.broadcast_to(own_labels[None, :], step_ids.shape)
    activation = cond_activation(
        step_ids.reshape(-1), class_ids.reshape(-1), class_table, w_freq, w_time
    )
    own_columns = jnp.dot(activation, w_ada, preferred_element_type=jnp.float32).astype(
        jnp.bfloat16
    )
    modulation = lax.all_to_all(own_columns, "tm", split_axis=0, concat_axis=1, tiled=True)
    point_count = local_steps * sample_count
    point_rows = by_sample.reshape(point_count, -1, LANES)
    own = jnp.stack([jnp.concatenate([w_qkv, w_proj.T], axis=1), w_fc1, w_fc2.T])
    parts = modulation.astype(jnp.float32).reshape(point_count, 8, -1)
    velocity_mid = denoise(point_rows, parts, w_patch, w_final, own, sizes)
    velocity_mid = velocity_mid.reshape(local_steps, sample_count, -1, LANES)
    velocity_out = lax.all_to_all(velocity_mid, "batch", split_axis=2, concat_axis=1, tiled=True)
    velocity_out = velocity_out.reshape(local_steps, sample_total, lat_block)
    velocity_float = velocity_out.astype(jnp.float32)
    summed = jnp.cumsum(velocity_float, axis=0)
    running = jnp.concatenate([jnp.zeros_like(summed[:1]), summed[:-1]], axis=0)
    block_sum = jnp.sum(velocity_float, axis=0)
    earlier_sum = entering(block_sum, "tm", add_pair, jnp.zeros_like(block_sum))
    latents_out = anchor[None] + (earlier_sum[None] + running) * (1.0 / STEPS)
    return (latents_out, velocity_out)


def chip_sizes(mesh):
    batch = mesh.shape["batch"]
    ys = 1
    while ys * ys * 4 <= batch:
        ys *= 2
    return mesh.shape["tm"] // CORES, ys, batch // ys


def solution(mesh):
    placed = (
        P("tm", None, "batch"),
        P(),
        P(),
        P(),
        P(),
        P(),
        P(),
        P(None, "tm"),
        P(),
        P("batch", "tm"),
        P("tm", "batch"),
        P("batch", "tm"),
        P("tm", "batch"),
        P(),
    )
    return jax.shard_map(
        functools.partial(local, chip_sizes(mesh)),
        mesh=mesh,
        in_specs=placed,
        out_specs=(P("tm", None, "batch"), P("tm", None, "batch")),
        check_vma=False,
    )
```

profile of v0, /device:TPU:0, one launch (start us, length us, event | category | flops | bytes accessed | tf_op | source)
XLA Modules:
  0.0 223.4 jit_solution(9603488631421270278)
XLA Ops:
  0.7 0.8 dynamic_slice.15
  1.5 0.1 reshape.203
  1.5 0.1 reshape.202
  1.6 0.8 dynamic-slice_add_fusion
  2.4 0.1 reshape.207
  2.5 0.1 fusion.9
  2.6 2.6 %gather_fusion = bf16[16,1152]{1,0:T(8,128)(2,1)S(1)} fusion(bf16[1001,1152]{1,0:T(8,128)(2,1)} %param.21, s32[1024]{0:T(1024)S(1)} %pad_clamp_fusion), kind=kCustom, calls=%fused_computation | custom fusion | bytes 73792 | tf_op jit(solution)/shard_map/jit(_take)/gather | solution.py:61
  5.2 0.2 fusion.11
  5.5 4.7 %convolution_convert_fusion = bf16[16,2304]{1,0:T(8,128)(2,1)S(1)} fusion(bf16[1152,2304]{1,0:T(8,128)(2,1)} %param.24, bf16[1152,1152]{1,0:T(8,128)(2,1)} %param.23, f32[16,1152]{1,0:T(8,128)S(1)} %fusion.11, bf16[16,1152]{1,0:T(8,128)(2,1)S(1)} %gather_fusion, pred[16]{0:T(512)(128)(4,1)S(1)} %compare_and_fusion), kind=kOutput, calls=%fused_computation.4 | convolution fusion | flops 127678464 | bytes 8146960 | tf_op jit(solution)/shard_map/dot_general | solution.py:473
  10.1 0.7 all_to_all.35
  10.8 4.2 %all-to-all-start.1 = ((bf16[4,4,2304]{2,1,0:T(4,128)(2,1)}), bf16[4,4,2304]{2,1,0:T(4,128)(2,1)S(1)}, u32[]{:S(2)}, u32[]{:S(2)}) async-start(bf16[4,4,2304]{2,1,0:T(4,128)(2,1)} %all_to_all.35), calls=%async_computation.1 | async-start | bytes 147456 | tf_op jit(solution)/shard_map/all_to_all | solution.py:476
  15.1 0.1 fusion.17
  15.2 0.1 reshape.225
  15.3 6.3 %all_gather.9 = f32[8,16,512]{2,1,0:T(8,128)S(1)} all-gather(f32[2,16,512]{2,1,0:T(8,128)S(1)} %copy-done.6), channel_id=1, replica_groups=mesh['tm'=4,'batch'=8] {'tm'}, dimensions={0}, use_global_device_ids=true | all-gather | bytes 327680 | tf_op jit(solution)/shard_map/all_gather | solution.py:451
  21.6 0.7 gather_fusion.2
  22.3 0.1 copy.47
  22.5 0.7 fusion.1
  23.2 0.1 maximum_bitcast_fusion
  23.3 1.1 pad_maximum_fusion.own_ref
  24.4 0.9 copy.52.w_final_ref
  25.3 0.6 gather_fusion.1
  26.0 6.3 %all-to-all-start = ((bf16[2,16,4,128]{3,2,0,1:T(4,128)(2,1)}), bf16[2,16,4,128]{3,2,0,1:T(4,128)(2,1)S(1)}, u32[]{:S(2)}, u32[]{:S(2)}) async-start(bf16[2,16,4,128]{3,2,0,1:T(4,128)(2,1)} %fusion.1), calls=%async_computation | async-start | bytes 65536 | tf_op jit(solution)/shard_map/all_to_all | solution.py:456
  32.4 0.7 reshape.208.mod_ref
  33.1 5.9 %all-to-all-done = bf16[2,16,4,128]{3,2,0,1:T(4,128)(2,1)S(1)} async-done(((bf16[2,16,4,128]{3,2,0,1:T(4,128)(2,1)}), bf16[2,16,4,128]{3,2,0,1:T(4,128)(2,1)S(1)}, u32[]{:S(2)}, u32[]{:S(2)}) %all-to-all-start) | async-done | bytes 32800 | tf_op jit(solution)/shard_map/all_to_all | solution.py:456
  39.0 0.6 copy.50
  39.6 166.0 %denoise.1 = bf16[4,32,128]{2,1,0:T(8,128)(2,1)} custom-call(bf16[4,32,128]{2,1,0:T(8,128)(2,1)} %bitcast.38, f32[4,8,1152]{2,1,0:T(8,128)} %reshape.208.mod_ref, bf16[16,1152]{1,0:T(8,128)(2,1)} %w_patch_ref.1, bf16[1152,16]{1,0:T(8,128)(2,1)} %copy.52.w_final_ref, f32[256,1152]{1,0:T(8,128)} %constant.86.clone.pos_ref, ...), custom_call_target="tpu_custom_call" | custom-call | tf_op jit(solution)/shard_map/denoise/pallas_call | solution.py:399
  205.6 1.4 copy.53
  207.0 3.3 %all-to-all-start.2 = ((bf16[2,2,32,128]{3,1,0,2:T(2,128)(2,1)}), bf16[2,2,32,128]{3,1,0,2:T(2,128)(2,1)S(1)}, u32[]{:S(2)}, u32[]{:S(2)}) async-start(bf16[2,2,32,128]{3,1,0,2:T(2,128)(2,1)} %copy.53), calls=%async_computation.2 | async-start | bytes 65536 | tf_op jit(solution)/shard_map/all_to_all | solution.py:483
  210.4 6.5 %all-to-all-done.2 = bf16[2,2,32,128]{3,1,0,2:T(2,128)(2,1)S(1)} async-done(((bf16[2,2,32,128]{3,1,0,2:T(2,128)(2,1)}), bf16[2,2,32,128]{3,1,0,2:T(2,128)(2,1)S(1)}, u32[]{:S(2)}, u32[]{:S(2)}) %all-to-all-start.2) | async-done | bytes 32800 | tf_op jit(solution)/shard_map/all_to_all | solution.py:483
  217.1 5.4 %all_gather.11 = f32[4,16,512]{2,1,0:T(8,128)S(1)} all-gather(f32[1,16,512]{2,1,0:T(8,128)S(1)} %all_gather.10), channel_id=1, replica_groups=mesh['tm'=4,'batch'=8] {'tm'}, dimensions={0}, use_global_device_ids=true | all-gather | bytes 163840 | tf_op jit(solution)/shard_map/all_gather | solution.py:24
  222.5 0.2 fusion.2
  222.7 0.6 multiply_add_fusion
  (45 shorter events, 0.5 us)
Async XLA Ops:
  0.6 4.6 %copy-start = (bf16[256,1152]{1,0:T(8,128)(2,1)S(1)}, bf16[256,1152]{1,0:T(8,128)(2,1)}, u32[]{:S(2)}) copy-start(bf16[256,1152]{1,0:T(8,128)(2,1)} %param.22) | copy-start | bytes 1769476
  5.4 9.6 %copy-start.8 = (s32[16]{0:T(128)S(1)}, s32[16]{0:T(128)}, u32[]{:S(2)}) copy-start(s32[16]{0:T(128)} %param.18) | copy-start | bytes 196
  5.4 9.9 %copy-start.6 = (f32[2,16,512]{2,1,0:T(8,128)S(1)}, f32[2,16,512]{2,1,0:T(8,128)}, u32[]{:S(2)}) copy-start(f32[2,16,512]{2,1,0:T(8,128)} %param.17) | copy-start | bytes 196612
  5.4 17.8 %copy-start.3 = (bf16[144,864]{1,0:T(8,128)(2,1)S(1)}, bf16[144,864]{1,0:T(8,128)(2,1)}, u32[]{:S(2)}) copy-start(bf16[144,864]{1,0:T(8,128)(2,1)} %param.26) | copy-start | bytes 746500
  5.4 17.7 %copy-start.5 = (bf16[288,144]{0,1:T(8,128)(2,1)S(1)}, bf16[288,144]{0,1:T(8,128)(2,1)}, u32[]{:S(2)}) copy-start(bf16[288,144]{0,1:T(8,128)(2,1)} %param.27) | copy-start | bytes 248836
  5.4 17.8 %copy-start.1 = (bf16[1152,144]{0,1:T(8,128)(2,1)S(1)}, bf16[1152,144]{0,1:T(8,128)(2,1)}, u32[]{:S(2)}) copy-start(bf16[1152,144]{0,1:T(8,128)(2,1)} %param.29) | copy-start | bytes 995332
  5.5 17.8 %copy-start.2 = (bf16[144,1152]{1,0:T(8,128)(2,1)S(1)}, bf16[144,1152]{1,0:T(8,128)(2,1)}, u32[]{:S(2)}) copy-start(bf16[144,1152]{1,0:T(8,128)(2,1)} %param.28) | copy-start | bytes 995332
  10.1 14.3 %copy-start.7 = (bf16[1152,16]{0,1:T(8,128)(2,1)S(1)}, bf16[1152,16]{0,1:T(8,128)(2,1)}, u32[]{:S(2)}) copy-start(bf16[1152,16]{0,1:T(8,128)(2,1)} %param.30) | copy-start | bytes 110596
  10.8 15.1 %all-to-all-start.1 = ((bf16[4,4,2304]{2,1,0:T(4,128)(2,1)}), bf16[4,4,2304]{2,1,0:T(4,128)(2,1)S(1)}, u32[]{:S(2)}, u32[]{:S(2)}) async-start(bf16[4,4,2304]{2,1,0:T(4,128)(2,1)} %all_to_all.35), calls=%async_computation.1 | async-start | bytes 147456 | tf_op jit(solution)/shard_map/all_to_all | solution.py:476
  26.0 13.0 %all-to-all-start = ((bf16[2,16,4,128]{3,2,0,1:T(4,128)(2,1)}), bf16[2,16,4,128]{3,2,0,1:T(4,128)(2,1)S(1)}, u32[]{:S(2)}, u32[]{:S(2)}) async-start(bf16[2,16,4,128]{3,2,0,1:T(4,128)(2,1)} %fusion.1), calls=%async_computation | async-start | bytes 65536 | tf_op jit(solution)/shard_map/all_to_all | solution.py:456
  207.0 10.0 %all-to-all-start.2 = ((bf16[2,2,32,128]{3,1,0,2:T(2,128)(2,1)}), bf16[2,2,32,128]{3,1,0,2:T(2,128)(2,1)S(1)}, u32[]{:S(2)}, u32[]{:S(2)}) async-start(bf16[2,2,32,128]{3,1,0,2:T(2,128)(2,1)} %copy.53), calls=%async_computation.2 | async-start | bytes 65536 | tf_op jit(solution)/shard_map/all_to_all | solution.py:483
  222.5 0.9 copy-start.4
where the time goes:
time: 224 us; the launch traced here: 223 us
  Pallas kernels  166 us (74%)
  starting transfers between devices  13.9 us (6%)
  waiting for transfers between devices  12.5 us (6%)
  blocking collectives  11.7 us (5%)
  local copies, waits for them, and re-layouts  9.66 us (4%)
  matrix products  4.86 us (2%)
  other arithmetic  3.97 us (2%)
    pallas_call x1, Pallas kernels, denoise(): pl.pallas_call(functools.partial(denoise_kernel, sizes, HEADS // shards,...  166 us
    all_to_all x1, waiting for transfers between devices, local(): lax.all_to_all(velocity_mid, 'batch', split_axis=2, concat_axis=1, tiled=...  6.55 us
    all_to_all x1, starting transfers between devices, local(): lax.all_to_all(points.astype(jnp.bfloat16).reshape(local_steps, sample_to...  6.33 us
    all_gather x1, blocking collectives, local(): whole = lax.all_gather(latents, 'tm', axis=0, tiled=True)  6.27 us
    all_to_all x1, waiting for transfers between devices, local(): lax.all_to_all(points.astype(jnp.bfloat16).reshape(local_steps, sample_to...  5.91 us
    all_gather x1, blocking collectives, entering(): gathered = lax.all_gather(part, axis)  5.42 us
    dot_general x1, matrix products, local(): jnp.dot(activation, w_ada, preferred_element_type=jnp.float32)  4.66 us
  transfers between devices with their start and end apart: 3, of which 2 were waited for; matrix products, arithmetic and copies ran while one was open for 2% of the time, Pallas kernels for 0%

commit v1 on v0

--- a/solution.py
+++ b/solution.py
@@ -17,17 +17,6 @@
 LANES = 128
 CORES = 2
 MESH = pl.DeviceIdType.MESH
-
-
-def entering(part, axis, combine, identity):
-    place = lax.axis_index(axis)
-    gathered = lax.all_gather(part, axis)
-    state = jnp.zeros_like(part) + jnp.asarray(identity, part.dtype)
-
-    def one(lap, state):
-        return combine(state, lax.dynamic_index_in_dim(gathered, lap, 0, False))
-
-    return lax.fori_loop(0, place, one, state)
 
 
 def layer_norm(values):
@@ -122,15 +111,16 @@
     def device(self, x, c, z, y):
         return {"tm": x * CORES + c, "batch": z * self.ys + y}
 
+    def tm_peers(self):
+        count = self.xs * CORES
+        return [{"tm": (self.tm + i) % count, "batch": self.batch} for i in range(1, count)]
+
+    def batch_peers(self):
+        count = self.ys * self.zs
+        return [{"tm": self.tm, "batch": (self.batch + i) % count} for i in range(1, count)]
+
     def peers(self):
-        out = [self.device(self.x, 1 - self.c, self.z, self.y)]
-        for step in range(1, self.zs):
-            out.append(self.device(self.x, self.c, self.along_z(step), self.y))
-        for step in range(1, self.xs):
-            out.append(self.device(self.peer(self.x, step, self.xs), self.c, self.z, self.y))
-        for step in range(1, self.ys):
-            out.append(self.device(self.x, self.c, self.z, self.peer(self.y, step, self.ys)))
-        return out
+        return self.tm_peers() + self.batch_peers()
 
     def greet(self):
         barrier = pltpu.get_barrier_semaphore()
@@ -242,28 +232,101 @@
                 pltpu.make_async_copy(region, region, self.send_sem.at[k, kind]).wait()
 
 
+class Exchange:
+    def __init__(self, index, sent, landed, send_sem, recv_sem, peers, axis):
+        self.sent, self.landed, self.peers, self.axis = sent, landed, peers, axis
+        self.send_sem, self.recv_sem = send_sem.at[index], recv_sem.at[index]
+
+    def start(self, me, source=None):
+        for peer in self.peers:
+            block = self.sent.at[peer[self.axis]] if source is None else source
+            pltpu.make_async_remote_copy(
+                src_ref=block,
+                dst_ref=self.landed.at[me],
+                send_sem=self.send_sem,
+                recv_sem=self.recv_sem,
+                device_id=peer,
+                device_id_type=MESH,
+            ).start()
+
+    def region(self):
+        return self.landed.at[pl.ds(0, len(self.peers))]
+
+    def arrived(self):
+        pltpu.make_async_copy(self.region(), self.region(), self.recv_sem).wait()
+
+    def left(self):
+        pltpu.make_async_copy(self.region(), self.region(), self.send_sem).wait()
+
+
 def denoise_kernel(
     sizes, head_count, head_size,
-    patch_ref, mod_ref, w_patch_ref, w_final_ref, pos_ref, own_ref, out_ref,
-    buf, tokens, normed, hidden, send_sem, z_sem, x_sem, y_sem, d_sem, p_sem,
+    shift_ref, latent_ref, act_ref, w_patch_ref, w_final_ref, pos_ref, own_ref, w_ada_hbm,
+    latent_out, velocity_out,
+    buf, tokens, normed, hidden, w_ada, window, sent_points, landed_points, sent_mod, landed_mod,
+    sent_velocity, landed_velocity, sent_sums, landed_sums, anchors, rows_in,
+    send_sem, z_sem, x_sem, y_sem, d_sem, p_sem, ex_send, ex_recv, ada_sem,
 ):
-    points, lane_rows, lanes = patch_ref.shape
+    steps, samples, lane_rows, lanes = latent_ref.shape
     patch_size, width = w_patch_ref.shape
     group = lanes // patch_size
-    token_count = lane_rows * group
-    shards = sizes[0] * CORES
+    shards, blocks = sizes[0] * CORES, sizes[1] * sizes[2]
+    own_samples = samples // blocks
+    points = steps * own_samples
     block_rows, block_width = own_ref.shape[1:]
+    columns = w_ada_hbm.shape[1]
+    fetch_ada = pltpu.make_async_copy(w_ada_hbm, w_ada, ada_sem)
+    fetch_ada.start()
     gather = Gather(sizes, own_ref, buf, send_sem, z_sem, x_sem, y_sem, d_sem, p_sem)
+    tm, batch = gather.tm, gather.batch
+    tm_peers, batch_peers = gather.tm_peers(), gather.batch_peers()
+    ex = functools.partial(Exchange, send_sem=ex_send, recv_sem=ex_recv)
+    latent_ex = ex(0, None, window, peers=tm_peers, axis="tm")
+    mod_ex = ex(1, sent_mod, landed_mod, peers=tm_peers, axis="tm")
+    point_ex = ex(2, sent_points, landed_points, peers=batch_peers, axis="batch")
+    velocity_ex = ex(3, sent_velocity, landed_velocity, peers=batch_peers, axis="batch")
+    sum_ex = ex(4, None, landed_sums, peers=tm_peers, axis="tm")
     gather.greet()
+    window[tm] = latent_ref[...]
     for k in range(3):
-        buf[k, gather.tm, gather.batch] = own_ref[k]
+        buf[k, tm, batch] = own_ref[k]
     gather.met()
+    latent_ex.start(tm, latent_ref)
     gather.own_out(0)
     for k in range(3):
         gather.to_z(k)
 
+    fetch_ada.wait()
+    mod = jnp.dot(act_ref[...], w_ada[...], preferred_element_type=jnp.float32)
+    mod = mod.astype(jnp.bfloat16).astype(jnp.float32)
+    for i in range(shards):
+        sent_mod[i] = mod[i * points : (i + 1) * points]
+    landed_mod[tm] = sent_mod[tm]
+    latent_ex.arrived()
+    mod_ex.start(tm)
+    for sample in range(samples):
+        shift = shift_ref[sample]
+        anchors[sample] = window[shift // steps, shift % steps, sample]
+        for step in range(steps):
+            source = jnp.minimum(tm * steps + step + shift, shards * steps - 1)
+            place = step * own_samples + sample % own_samples
+            sent_points[sample // own_samples, place] = window[
+                source // steps, source % steps, sample
+            ]
+    landed_points[batch] = sent_points[batch]
+    point_ex.start(batch)
+    gather.from_z(0, 1)
+    mod_ex.arrived()
+    point_ex.arrived()
+
     def part(point, index):
-        return mod_ref[point, pl.ds(index, 1), :]
+        pieces, at = [], index * width
+        while at < (index + 1) * width:
+            start = at % columns
+            size = min(columns - start, (index + 1) * width - at)
+            pieces.append(landed_mod[at // columns, pl.ds(point, 1), start : start + size])
+            at += size
+        return pieces[0] if len(pieces) == 1 else jnp.concatenate(pieces, axis=1)
 
     def modulated(values, point, index):
         return (layer_norm(values) * (1.0 + part(point, index + 1)) + part(point, index)).astype(
@@ -271,7 +334,9 @@
         )
 
     def enter(point, carry):
-        flat = patch_ref[point]
+        for block in range(blocks):
+            rows_in[block * lane_rows : (block + 1) * lane_rows, :] = landed_points[block, point]
+        flat = rows_in[...].astype(jnp.bfloat16)
         pieces = [flat[:, k * patch_size : (k + 1) * patch_size] for k in range(group)]
         value = jnp.dot(
             jnp.concatenate(pieces, axis=0), w_patch_ref[...], preferred_element_type=jnp.float32
@@ -284,7 +349,7 @@
     lax.fori_loop(0, points, enter, 0)
 
     for step in range(sizes[2]):
-        if step:
+        if step > 1:
             gather.from_z(0, step)
         if step > 1:
             gather.from_xy(0, step - 2)
@@ -375,53 +440,97 @@
     def leave(point, carry):
         final_in = modulated(tokens[point], point, 6)
         value = jnp.dot(final_in, w_final_ref[...], preferred_element_type=jnp.float32)
-        pieces = [value[k * lane_rows : (k + 1) * lane_rows, :] for k in range(group)]
-        out_ref[point] = jnp.concatenate(pieces, axis=1).astype(jnp.bfloat16)
+        flat_rows = blocks * lane_rows
+        pieces = [value[k * flat_rows : (k + 1) * flat_rows, :] for k in range(group)]
+        flat = jnp.concatenate(pieces, axis=1).astype(jnp.bfloat16).astype(jnp.float32)
+        for block in range(blocks):
+            sent_velocity[block, point] = flat[block * lane_rows : (block + 1) * lane_rows]
         return carry
 
     lax.fori_loop(0, points, leave, 0)
+    landed_velocity[batch] = sent_velocity[batch]
+    velocity_ex.start(batch)
+    velocity_ex.arrived()
+
+    def step_velocity(step):
+        value = landed_velocity[:, step * own_samples : (step + 1) * own_samples]
+        return value.reshape(samples, lane_rows, lanes)
+
+    total = step_velocity(0)
+    for step in range(1, steps):
+        total = total + step_velocity(step)
+    sent_sums[...] = total
+    sum_ex.start(tm, sent_sums)
+    for step in range(steps):
+        velocity_out[step] = step_velocity(step)
+    sum_ex.arrived()
+    running = jnp.zeros_like(total)
+    for i in range(shards):
+        running = running + jnp.where(i < tm, landed_sums[i], 0.0)
+    for step in range(steps):
+        latent_out[step] = anchors[...] + running * (1.0 / STEPS)
+        running = running + step_velocity(step)
+    for exchange in (latent_ex, mod_ex, point_ex, velocity_ex, sum_ex):
+        exchange.left()
     for k in range(3):
         gather.all_left(k)
 
 
-def denoise(patch_rows, modulation, w_patch, w_final, own, sizes):
-    points, lane_rows, lanes = patch_rows.shape
+def denoise(shifts, latents, activation, w_ada, w_patch, w_final, own, sizes):
+    steps, samples, lane_rows, lanes = latents.shape
     patch_size, width = w_patch.shape
     group = lanes // patch_size
-    token_count = lane_rows * group
     xs, ys, zs = sizes
     shards, blocks = xs * CORES, ys * zs
+    token_count = blocks * lane_rows * group
+    points = steps * samples // blocks
     block_rows, block_width = own.shape[1:]
     pos = jnp.asarray(position_table(token_count, group))
     dma = pltpu.SemaphoreType.DMA
     head_size = width // HEADS
     vmem = pl.BlockSpec(memory_space=pltpu.VMEM)
+    smem = pl.BlockSpec(memory_space=pltpu.SMEM)
+    result = jax.ShapeDtypeStruct(latents.shape, jnp.float32)
+    pieces = pltpu.VMEM((blocks, points, lane_rows, lanes), jnp.float32)
+    sums = (samples, lane_rows, lanes)
+    mod = pltpu.VMEM((shards, points, w_ada.shape[1]), jnp.float32)
     return pl.pallas_call(
         functools.partial(denoise_kernel, sizes, HEADS // shards, head_size),
-        out_shape=jax.ShapeDtypeStruct(patch_rows.shape, jnp.bfloat16),
-        in_specs=[vmem] * 6,
-        out_specs=vmem,
+        out_shape=(result, result),
+        in_specs=[smem] + [vmem] * 6 + [pl.BlockSpec(memory_space=pl.ANY)],
+        out_specs=(vmem, vmem),
         scratch_shapes=[
             pltpu.VMEM((3, shards, blocks, block_rows, block_width), jnp.bfloat16),
             pltpu.VMEM((points, token_count, width), jnp.float32),
             pltpu.VMEM((points, token_count, width), jnp.bfloat16),
             pltpu.VMEM((shards, points, token_count, block_width), jnp.bfloat16),
+            pltpu.VMEM(w_ada.shape, jnp.bfloat16),
+            pltpu.VMEM((shards, *latents.shape), jnp.float32),
+            pieces,
+            pieces,
+            mod,
+            mod,
+            pieces,
+            pieces,
+            pltpu.VMEM(sums, jnp.float32),
+            pltpu.VMEM((shards, *sums), jnp.float32),
+            pltpu.VMEM(sums, jnp.float32),
+            pltpu.VMEM((blocks * lane_rows, lanes), jnp.float32),
             dma((3, 5)),
             dma((3, zs)),
             dma((3, zs * xs)),
             dma((3, zs * ys)),
             dma((3, xs)),
             dma((3, xs)),
+            dma((5,)),
+            dma((5,)),
+            dma,
         ],
         compiler_params=pltpu.CompilerParams(
-            collective_id=0, has_side_effects=True, vmem_limit_bytes=66_000_000
+            collective_id=0, has_side_effects=True, vmem_limit_bytes=67_000_000
         ),
         name="denoise",
-    )(patch_rows, modulation, w_patch, w_final, pos, own)
-
-
-def add_pair(earlier, later):
-    return earlier + later
+    )(shifts, latents, activation, w_patch, w_final, pos, own, w_ada)
 
 
 def local(
@@ -441,26 +550,10 @@
     w_fc2,
     w_final,
 ):
-    tm_count = lax.axis_size("tm")
-    tm_index = lax.axis_index("tm")
     batch_index = lax.axis_index("batch")
-    local_steps = latents.shape[0]
-    window = local_steps * tm_count
-    sample_total, lat_block = latents.shape[1:]
-    lane_rows = lat_block // LANES
-    whole = lax.all_gather(latents, "tm", axis=0, tiled=True)
-    local_positions = tm_index * local_steps + jnp.arange(local_steps, dtype=jnp.int32)[:, None]
-    source_rows = jnp.minimum(local_positions + shifts[None, :], window - 1)
-    points = jnp.take_along_axis(whole, source_rows[:, :, None], axis=0)
-    anchor = jnp.take_along_axis(whole, shifts[None, :, None], axis=0)[0]
-    by_sample = lax.all_to_all(
-        points.astype(jnp.bfloat16).reshape(local_steps, sample_total, lane_rows, LANES),
-        "batch",
-        split_axis=1,
-        concat_axis=2,
-        tiled=True,
-    )
-    sample_count = by_sample.shape[1]
+    local_steps, sample_total, lat_block = latents.shape
+    window = local_steps * lax.axis_size("tm")
+    sample_count = sample_total // lax.axis_size("batch")
     own_shifts = lax.dynamic_slice_in_dim(shifts, batch_index * sample_count, sample_count)
     own_starts = lax.dynamic_slice_in_dim(starts, batch_index * sample_count, sample_count)
     own_labels = lax.dynamic_slice_in_dim(labels, batch_index * sample_count, sample_count)
@@ -470,25 +563,13 @@
     activation = cond_activation(
         step_ids.reshape(-1), class_ids.reshape(-1), class_table, w_freq, w_time
     )
-    own_columns = jnp.dot(activation, w_ada, preferred_element_type=jnp.float32).astype(
-        jnp.bfloat16
-    )
-    modulation = lax.all_to_all(own_columns, "tm", split_axis=0, concat_axis=1, tiled=True)
-    point_count = local_steps * sample_count
-    point_rows = by_sample.reshape(point_count, -1, LANES)
     own = jnp.stack([jnp.concatenate([w_qkv, w_proj.T], axis=1), w_fc1, w_fc2.T])
-    parts = modulation.astype(jnp.float32).reshape(point_count, 8, -1)
-    velocity_mid = denoise(point_rows, parts, w_patch, w_final, own, sizes)
-    velocity_mid = velocity_mid.reshape(local_steps, sample_count, -1, LANES)
-    velocity_out = lax.all_to_all(velocity_mid, "batch", split_axis=2, concat_axis=1, tiled=True)
-    velocity_out = velocity_out.reshape(local_steps, sample_total, lat_block)
-    velocity_float = velocity_out.astype(jnp.float32)
-    summed = jnp.cumsum(velocity_float, axis=0)
-    running = jnp.concatenate([jnp.zeros_like(summed[:1]), summed[:-1]], axis=0)
-    block_sum = jnp.sum(velocity_float, axis=0)
-    earlier_sum = entering(block_sum, "tm", add_pair, jnp.zeros_like(block_sum))
-    latents_out = anchor[None] + (earlier_sum[None] + running) * (1.0 / STEPS)
-    return (latents_out, velocity_out)
+    rows = latents.reshape(local_steps, sample_total, lat_block // LANES, LANES)
+    latents_out, velocity = denoise(shifts, rows, activation, w_ada, w_patch, w_final, own, sizes)
+    return (
+        latents_out.reshape(latents.shape),
+        velocity.astype(jnp.bfloat16).reshape(latents.shape),
+    )
 
 
 def chip_sizes(mesh):

time: 224 us -> 253 us (1.13)
  Pallas kernels: 166 us -> 238 us
  starting transfers between devices: 13.9 us -> 0 us
  waiting for transfers between devices: 12.5 us -> 0 us
  blocking collectives: 11.7 us -> 0 us
    pallas_call x1, Pallas kernels: 166 us -> 238 us  [denoise(): pl.pallas_call(functools.partial(denoise_kernel, sizes, HEADS // shards,...]
    all_to_all x3 -> x0, starting transfers between devices: 13.9 us -> none  [the longest x1 6.33 us: local(): lax.all_to_all(points.astype(jnp.bfloat16).reshape(local_steps, sample_to...]
    all_to_all x3 -> x0, waiting for transfers between devices: 12.5 us -> none  [the longest x1 6.55 us: local(): lax.all_to_all(velocity_mid, 'batch', split_axis=2, concat_axis=1, tiled=...]
    all_gather x2 -> x0, blocking collectives: 11.7 us -> none  [the longest x1 6.27 us: local(): whole = lax.all_gather(latents, 'tm', axis=0, tiled=True)]
  transfers between devices with their start and end apart: 3 -> 0, of which waited for: 2 -> 0; matrix products, arithmetic and copies ran while one was open for 2% -> 0% of each run, Pallas kernels for 0% -> 0%
where the time goes in v1:
time: 253 us; the launch traced here: 252 us
  Pallas kernels  238 us (94%)
  local copies, waits for them, and re-layouts  7.34 us (3%)
  matrix products  3.2 us (1%)
  other arithmetic  2.96 us (1%)
    pallas_call x1, Pallas kernels, denoise(): pl.pallas_call(functools.partial(denoise_kernel, sizes, HEADS // shards,...  238 us

profile of v1, /device:TPU:0, one launch (start us, length us, event | category | flops | bytes accessed | tf_op | source)
XLA Modules:
  0.0 252.3 jit_solution(12523753443156731219)
XLA Ops:
  0.6 0.0 copy-start.3
  0.6 0.0 copy-start.2
  0.7 0.0 copy-start.1
  0.7 0.0 copy-start
  0.7 0.8 dynamic_slice.11
  1.5 0.1 reshape.83
  1.6 2.6 %gather_fusion = bf16[16,1152]{1,0:T(8,128)(2,1)S(1)} fusion(bf16[1001,1152]{1,0:T(8,128)(2,1)} %param.19, s32[1024]{0:T(1024)S(1)} %pad_clamp_fusion), kind=kCustom, calls=%fused_computation | custom fusion | bytes 73792 | tf_op jit(solution)/shard_map/jit(_take)/gather | solution.py:50
  4.2 0.8 dynamic-slice_add_fusion
  4.9 0.1 reshape.87
  5.0 0.1 fusion.1
  5.2 0.1 reshape.82
  5.3 0.0 copy-start.5
  5.3 0.0 copy-start.4
  5.3 3.2 %multiply_convert_fusion.act_ref = bf16[16,1152]{1,0:T(8,128)(2,1)} fusion(bf16[1152,1152]{1,0:T(8,128)(2,1)} %param.21, bf16[16,1152]{1,0:T(8,128)(2,1)S(1)} %gather_fusion, pred[16]{0:T(512)(128)(4,1)S(1)} %compare_and_fusion, bf16[256,1152]{1,0:T(8,128)(2,1)} %param.20, bf16[16,128]{1,0:T(8,128)(2,1)S(1)} %get-tuple-element.7, ...), kind=kOutput, calls=%fused_computation.4 | convolution fusion | flops 52160512 | bytes 3325968 | tf_op jit(solution)/shard_map/dot_general | solution.py:50
  8.5 0.0 copy-done.3
  8.5 0.0 copy-done.2
  8.5 0.1 maximum_bitcast_fusion
  8.6 0.0 copy-done.1
  8.6 0.0 copy-done
  8.6 1.1 pad_maximum_fusion.own_ref
  9.7 0.0 copy-done.5
  9.7 0.9 copy.18.w_final_ref
  10.6 0.0 copy-done.4
  10.6 0.7 reshape.81.latent_ref
  11.2 238.1 %denoise.1 = (f32[2,16,4,128]{3,2,1,0:T(4,128)}, f32[2,16,4,128]{3,2,1,0:T(4,128)}) custom-call(s32[16]{0:T(128)} %shift_ref.1, f32[2,16,4,128]{3,2,1,0:T(4,128)} %reshape.81.latent_ref, bf16[16,1152]{1,0:T(8,128)(2,1)} %multiply_convert_fusion.act_ref, bf16[16,1152]{1,0:T(8,128)(2,1)} %w_patch_ref.1, bf16[1152,16]{1,0:T(8,128)(2,1)} %copy.18.w_final_ref, ...), custom_call_target="tpu_custom_call" | custom-call | tf_op jit(solution)/shard_map/denoise/pallas_call | solution.py:497
  249.3 1.5 reshape.84
  250.8 0.9 convert_element_type.25
  251.7 0.6 reshape.85
  (6 shorter events, 0.1 us)
Async XLA Ops:
  0.6 7.8 %copy-start.3 = (bf16[288,144]{0,1:T(8,128)(2,1)S(1)}, bf16[288,144]{0,1:T(8,128)(2,1)}, u32[]{:S(2)}) copy-start(bf16[288,144]{0,1:T(8,128)(2,1)} %param.25) | copy-start | bytes 248836
  0.6 7.8 %copy-start.2 = (bf16[144,864]{1,0:T(8,128)(2,1)S(1)}, bf16[144,864]{1,0:T(8,128)(2,1)}, u32[]{:S(2)}) copy-start(bf16[144,864]{1,0:T(8,128)(2,1)} %param.24) | copy-start | bytes 746500
  0.7 7.9 %copy-start.1 = (bf16[144,1152]{1,0:T(8,128)(2,1)S(1)}, bf16[144,1152]{1,0:T(8,128)(2,1)}, u32[]{:S(2)}) copy-start(bf16[144,1152]{1,0:T(8,128)(2,1)} %param.26) | copy-start | bytes 995332
  0.7 7.9 %copy-start = (bf16[1152,144]{0,1:T(8,128)(2,1)S(1)}, bf16[1152,144]{0,1:T(8,128)(2,1)}, u32[]{:S(2)}) copy-start(bf16[1152,144]{0,1:T(8,128)(2,1)} %param.27) | copy-start | bytes 995332
  5.3 4.4 %copy-start.5 = (bf16[1152,16]{0,1:T(8,128)(2,1)S(1)}, bf16[1152,16]{0,1:T(8,128)(2,1)}, u32[]{:S(2)}) copy-start(bf16[1152,16]{0,1:T(8,128)(2,1)} %param.28) | copy-start | bytes 110596
  5.3 5.3 %copy-start.4 = (f32[2,16,512]{2,1,0:T(8,128)S(1)}, f32[2,16,512]{2,1,0:T(8,128)}, u32[]{:S(2)}) copy-start(f32[2,16,512]{2,1,0:T(8,128)} %param.15) | copy-start | bytes 196612

commit v2 on v1

--- a/solution.py
+++ b/solution.py
@@ -38,19 +38,12 @@
         [np.sin(col_angle), np.cos(col_angle), np.sin(row_angle), np.cos(row_angle)], axis=1
     ).astype(np.float32)
 
-def cond_activation(step_ids, class_ids, class_table, w_freq, w_time):
+def step_table(count):
     half_freq = FREQ // 2
-    freqs = jnp.exp(-math.log(10000.0) * jnp.arange(half_freq, dtype=jnp.float32) / half_freq)
-    tvalue = 1000.0 * (1.0 - step_ids.astype(jnp.float32) / STEPS)
-    angles = tvalue[:, None] * freqs[None, :]
-    embedded = jnp.concatenate([jnp.cos(angles), jnp.sin(angles)], axis=1).astype(jnp.bfloat16)
-    hidden_time = jax.nn.silu(jnp.dot(embedded, w_freq, preferred_element_type=jnp.float32)).astype(
-        jnp.bfloat16
-    )
-    condition = jnp.dot(hidden_time, w_time, preferred_element_type=jnp.float32) + jnp.take(
-        class_table, class_ids, axis=0
-    ).astype(jnp.float32)
-    return jax.nn.silu(condition).astype(jnp.bfloat16)
+    freqs = np.exp(-math.log(10000.0) * np.arange(half_freq, dtype=np.float32) / half_freq)
+    tvalue = 1000.0 * (1.0 - np.arange(count, dtype=np.float32) / np.float32(STEPS))
+    angles = tvalue.astype(np.float32)[:, None] * freqs.astype(np.float32)[None, :]
+    return np.concatenate([np.cos(angles), np.sin(angles)], axis=1).astype(np.float32)
 
 
 def times_transposed(left, right):
@@ -153,9 +146,9 @@
         device = self.device(self.x, 1 - self.c, self.z, self.y)
         self.send(k, 0, block, self.whole, device, self.p_sem.at[k, block[0]], own)
 
-    def to_z(self, k):
+    def to_z(self, k, steps):
         block = (self.x, self.z, self.y)
-        for step in range(1, self.zs):
+        for step in steps:
             device = self.device(self.x, self.c, self.along_z(step), self.y)
             self.send(k, 1, block, self.whole, device, self.z_sem.at[k, self.z], True)
 
@@ -261,9 +254,9 @@
 
 def denoise_kernel(
     sizes, head_count, head_size,
-    shift_ref, latent_ref, act_ref, w_patch_ref, w_final_ref, pos_ref, own_ref, w_ada_hbm,
-    latent_out, velocity_out,
-    buf, tokens, normed, hidden, w_ada, window, sent_points, landed_points, sent_mod, landed_mod,
+    shift_ref, start_ref, label_ref, latent_ref, table_ref, w_patch_ref, w_final_ref, pos_ref, own_ref,
+    class_hbm, w_freq_hbm, w_time_hbm, w_ada_hbm, latent_out, velocity_out,
+    buf, tokens, normed, hidden, classes, w_freq, w_time, w_ada, features, window, sent_points, landed_points, sent_mod, landed_mod,
     sent_velocity, landed_velocity, sent_sums, landed_sums, anchors, rows_in,
     send_sem, z_sem, x_sem, y_sem, d_sem, p_sem, ex_send, ex_recv, ada_sem,
 ):
@@ -275,8 +268,14 @@
     points = steps * own_samples
     block_rows, block_width = own_ref.shape[1:]
     columns = w_ada_hbm.shape[1]
-    fetch_ada = pltpu.make_async_copy(w_ada_hbm, w_ada, ada_sem)
-    fetch_ada.start()
+    fetches = [
+        pltpu.make_async_copy(source, target, ada_sem.at[i])
+        for i, (source, target) in enumerate(
+            [(w_freq_hbm, w_freq), (class_hbm, classes), (w_time_hbm, w_time), (w_ada_hbm, w_ada)]
+        )
+    ]
+    for fetch in fetches:
+        fetch.start()
     gather = Gather(sizes, own_ref, buf, send_sem, z_sem, x_sem, y_sem, d_sem, p_sem)
     tm, batch = gather.tm, gather.batch
     tm_peers, batch_peers = gather.tm_peers(), gather.batch_peers()
@@ -293,17 +292,37 @@
     gather.met()
     latent_ex.start(tm, latent_ref)
     gather.own_out(0)
-    for k in range(3):
-        gather.to_z(k)
-
-    fetch_ada.wait()
-    mod = jnp.dot(act_ref[...], w_ada[...], preferred_element_type=jnp.float32)
+    gather.to_z(0, range(1, sizes[2]))
+
+    row_count = shards * points
+    row_ids = lax.broadcasted_iota(jnp.int32, (row_count, classes.shape[0]), 0)
+    class_ids = lax.broadcasted_iota(jnp.int32, (row_count, classes.shape[0]), 1)
+    wanted = jnp.zeros_like(row_ids)
+    for place in range(own_samples):
+        sample = batch * own_samples + place
+        wanted = jnp.where(row_ids % own_samples == place, label_ref[sample], wanted)
+        for position in range(shards * steps):
+            step_id = start_ref[sample] + shift_ref[sample] + position
+            row = position * own_samples + place
+            features[row : row + 1, :] = table_ref[pl.ds(step_id, 1), :]
+    chosen = jnp.where(class_ids == wanted, 1.0, 0.0).astype(jnp.bfloat16)
+    for fetch in fetches[:3]:
+        fetch.wait()
+    hidden_time = jnp.dot(
+        features[...].astype(jnp.bfloat16), w_freq[...], preferred_element_type=jnp.float32
+    )
+    hidden_time = jax.nn.silu(hidden_time).astype(jnp.bfloat16)
+    condition = jnp.dot(hidden_time, w_time[...], preferred_element_type=jnp.float32)
+    condition = condition + jnp.dot(chosen, classes[...], preferred_element_type=jnp.float32)
+    activation = jax.nn.silu(condition).astype(jnp.bfloat16)
+    fetches[3].wait()
+    mod = jnp.dot(activation, w_ada[...], preferred_element_type=jnp.float32)
     mod = mod.astype(jnp.bfloat16).astype(jnp.float32)
     for i in range(shards):
         sent_mod[i] = mod[i * points : (i + 1) * points]
     landed_mod[tm] = sent_mod[tm]
+    mod_ex.start(tm)
     latent_ex.arrived()
-    mod_ex.start(tm)
     for sample in range(samples):
         shift = shift_ref[sample]
         anchors[sample] = window[shift // steps, shift % steps, sample]
@@ -315,9 +334,8 @@
             ]
     landed_points[batch] = sent_points[batch]
     point_ex.start(batch)
-    gather.from_z(0, 1)
-    mod_ex.arrived()
-    point_ex.arrived()
+    for k in range(1, 3):
+        gather.to_z(k, range(1, sizes[2]))
 
     def part(point, index):
         pieces, at = [], index * width
@@ -346,16 +364,18 @@
         normed[point] = modulated(value, point, 0)
         return carry
 
-    lax.fori_loop(0, points, enter, 0)
-
-    for step in range(sizes[2]):
-        if step > 1:
-            gather.from_z(0, step)
-        if step > 1:
-            gather.from_xy(0, step - 2)
-    gather.from_xy(0, max(sizes[2] - 2, 0))
-    if sizes[2] > 1:
-        gather.from_xy(0, sizes[2] - 1)
+    last = sizes[2] - 1
+    for step in range(1, last):
+        gather.from_z(0, step)
+        gather.from_xy(0, step - 1)
+    mod_ex.arrived()
+    point_ex.arrived()
+    lax.fori_loop(0, points // 2, enter, 0)
+    if last:
+        gather.from_z(0, last)
+    lax.fori_loop(points // 2, points, enter, 0)
+    for step in range(max(last - 1, 0), sizes[2]):
+        gather.from_xy(0, step)
     gather.own_out(1)
 
     def weights(k, shard):
@@ -411,7 +431,7 @@
     half = CORES / shards
     sweep(
         0,
-        [(half, functools.partial(gather.from_diagonal, 0))] + relay(1, 0.1, 0.8, 2),
+        [(half, functools.partial(gather.from_diagonal, 0))] + relay(1, 0.1, 0.95, 2),
         attention_step,
     )
 
@@ -439,7 +459,7 @@
 
     def leave(point, carry):
         final_in = modulated(tokens[point], point, 6)
-        value = jnp.dot(final_in, w_final_ref[...], preferred_element_type=jnp.float32)
+        value = times_transposed(final_in, w_final_ref[...])
         flat_rows = blocks * lane_rows
         pieces = [value[k * flat_rows : (k + 1) * flat_rows, :] for k in range(group)]
         flat = jnp.concatenate(pieces, axis=1).astype(jnp.bfloat16).astype(jnp.float32)
@@ -476,7 +496,7 @@
         gather.all_left(k)
 
 
-def denoise(shifts, latents, activation, w_ada, w_patch, w_final, own, sizes):
+def denoise(sizes, whole, scalars, latents, w_patch, w_final, own, conditioning):
     steps, samples, lane_rows, lanes = latents.shape
     patch_size, width = w_patch.shape
     group = lanes // patch_size
@@ -493,18 +513,21 @@
     result = jax.ShapeDtypeStruct(latents.shape, jnp.float32)
     pieces = pltpu.VMEM((blocks, points, lane_rows, lanes), jnp.float32)
     sums = (samples, lane_rows, lanes)
-    mod = pltpu.VMEM((shards, points, w_ada.shape[1]), jnp.float32)
+    columns = conditioning[-1].shape[1]
+    mod = pltpu.VMEM((shards, points, columns), jnp.float32)
+    table = jnp.asarray(step_table(whole))
     return pl.pallas_call(
         functools.partial(denoise_kernel, sizes, HEADS // shards, head_size),
         out_shape=(result, result),
-        in_specs=[smem] + [vmem] * 6 + [pl.BlockSpec(memory_space=pl.ANY)],
+        in_specs=[smem] * 3 + [vmem] * 6 + [pl.BlockSpec(memory_space=pl.ANY)] * 4,
         out_specs=(vmem, vmem),
         scratch_shapes=[
             pltpu.VMEM((3, shards, blocks, block_rows, block_width), jnp.bfloat16),
             pltpu.VMEM((points, token_count, width), jnp.float32),
             pltpu.VMEM((points, token_count, width), jnp.bfloat16),
             pltpu.VMEM((shards, points, token_count, block_width), jnp.bfloat16),
-            pltpu.VMEM(w_ada.shape, jnp.bfloat16),
+            *(pltpu.VMEM(value.shape, jnp.bfloat16) for value in conditioning),
+            pltpu.VMEM((shards * points, FREQ), jnp.float32),
             pltpu.VMEM((shards, *latents.shape), jnp.float32),
             pieces,
             pieces,
@@ -524,13 +547,13 @@
             dma((3, xs)),
             dma((5,)),
             dma((5,)),
-            dma,
+            dma((4,)),
         ],
         compiler_params=pltpu.CompilerParams(
             collective_id=0, has_side_effects=True, vmem_limit_bytes=67_000_000
         ),
         name="denoise",
-    )(shifts, latents, activation, w_patch, w_final, pos, own, w_ada)
+    )(*scalars, latents, table, w_patch, w_final, pos, own, *conditioning)
 
 
 def local(
@@ -550,22 +573,15 @@
     w_fc2,
     w_final,
 ):
-    batch_index = lax.axis_index("batch")
     local_steps, sample_total, lat_block = latents.shape
-    window = local_steps * lax.axis_size("tm")
-    sample_count = sample_total // lax.axis_size("batch")
-    own_shifts = lax.dynamic_slice_in_dim(shifts, batch_index * sample_count, sample_count)
-    own_starts = lax.dynamic_slice_in_dim(starts, batch_index * sample_count, sample_count)
-    own_labels = lax.dynamic_slice_in_dim(labels, batch_index * sample_count, sample_count)
-    window_positions = jnp.arange(window, dtype=jnp.int32)[:, None]
-    step_ids = (own_starts + own_shifts)[None, :] + window_positions
-    class_ids = jnp.broadcast_to(own_labels[None, :], step_ids.shape)
-    activation = cond_activation(
-        step_ids.reshape(-1), class_ids.reshape(-1), class_table, w_freq, w_time
-    )
     own = jnp.stack([jnp.concatenate([w_qkv, w_proj.T], axis=1), w_fc1, w_fc2.T])
     rows = latents.reshape(local_steps, sample_total, lat_block // LANES, LANES)
-    latents_out, velocity = denoise(shifts, rows, activation, w_ada, w_patch, w_final, own, sizes)
+    scalars = (shifts, starts, labels)
+    conditioning = (class_table, w_freq, w_time, w_ada)
+    whole = STEPS + 2 * local_steps * lax.axis_size("tm")
+    latents_out, velocity = denoise(
+        sizes, whole, scalars, rows, w_patch, w_final.T, own, conditioning
+    )
     return (
         latents_out.reshape(latents.shape),
         velocity.astype(jnp.bfloat16).reshape(latents.shape),

time: 253 us -> 189 us (0.75)
  Pallas kernels: 238 us -> 181 us
  local copies, waits for them, and re-layouts: 7.34 us -> 2.79 us
  matrix products: 3.2 us -> 0 us
    pallas_call x1, Pallas kernels: 238 us -> 181 us  [denoise(): pl.pallas_call(functools.partial(denoise_kernel, sizes, HEADS // shards,...]
    dot_general x1 -> x0, matrix products: 3.2 us -> none  [cond_activation(): jnp.dot(hidden_time, w_time, preferred_element_type=jnp.float32)]
    gather x1 -> x0, local copies, waits for them, and re-layouts: 2.58 us -> none  [cond_activation(): jnp.take(class_table, class_ids, axis=0).astype(jnp.float32)]
where the time goes in v2:
time: 189 us
  Pallas kernels  181 us (96%)
  other arithmetic  4.15 us (2%)
  local copies, waits for them, and re-layouts  2.79 us (1%)
    pallas_call x1, Pallas kernels, denoise(): pl.pallas_call(functools.partial(denoise_kernel, sizes, HEADS // shards,...  181 us

profile of v2, /device:TPU:0, one launch (start us, length us, event | category | flops | bytes accessed | tf_op | source)
XLA Modules:
  0.0 189.0 jit_solution(17575656625431246606)
XLA Ops:
  0.6 0.0 copy-start
  0.6 1.1 maximum_bitcast_fusion
  1.8 2.2 %pad_maximum_fusion.own_ref = bf16[3,144,1152]{2,1,0:T(8,128)(2,1)} fusion(bf16[1,144,1152]{2,1,0:T(8,128)(2,1)} %bitcast.8, bf16[1,144,1152]{2,1,0:T(8,128)(2,1)} %bitcast.9, bf16[1,144,1152]{2,1,0:T(8,128)(2,1)S(1)} %maximum_bitcast_fusion), kind=kLoop, calls=%fused_computation | loop fusion | flops 995328 | bytes 1990656 | tf_op jit(solution)/shard_map/stack | solution.py:577
  3.9 0.0 copy-done
  3.9 0.7 reshape.13.latent_ref
  4.6 181.4 %denoise.1 = (f32[2,16,4,128]{3,2,1,0:T(4,128)}, f32[2,16,4,128]{3,2,1,0:T(4,128)}) custom-call(s32[16]{0:T(128)} %shift_ref.1, s32[16]{0:T(128)} %start_ref.1, s32[16]{0:T(128)} %label_ref.1, f32[2,16,4,128]{3,2,1,0:T(4,128)} %reshape.13.latent_ref, f32[34,256]{1,0:T(8,128)} %constant.5.clone.table_ref, bf16[16,1152]{1,0:T(8,128)(2,1)} %w_patch_ref.1, ...), custom_call_target="tpu_custom_call" | custom-call | tf_op jit(solution)/shard_map/denoise/pallas_call | solution.py:519
  186.0 1.5 reshape.14
  187.5 0.9 convert_element_type.3
  188.3 0.6 reshape.15
Async XLA Ops:
  0.6 3.3 %copy-start = (f32[2,16,512]{2,1,0:T(8,128)S(1)}, f32[2,16,512]{2,1,0:T(8,128)}, u32[]{:S(2)}) copy-start(f32[2,16,512]{2,1,0:T(8,128)} %param.16) | copy-start | bytes 196612

commit v3 on v2

--- a/solution.py
+++ b/solution.py
@@ -375,8 +375,9 @@
         gather.from_z(0, last)
     lax.fori_loop(points // 2, points, enter, 0)
     for step in range(max(last - 1, 0), sizes[2]):
+        if step == last:
+            gather.own_out(1)
         gather.from_xy(0, step)
-    gather.own_out(1)
 
     def weights(k, shard):
         return buf[k, shard].reshape(sizes[1] * sizes[2] * block_rows, block_width)
@@ -385,15 +386,15 @@
         x = (gather.x + turn // CORES) % sizes[0]
         return x, x * CORES + (gather.c + turn % CORES) % CORES
 
-    total_steps = shards * points
-
-    def sweep(k, events, body):
+    def sweep(k, events, body, together=1):
+        turns = points // together
+        total_steps = shards * turns
         at = {}
         for share, event in events:
             at.setdefault(int(share * total_steps), []).append(event)
 
         def one(step, carry):
-            turn, point = step // points, step % points
+            turn, point = step // turns, step % turns * together
             x, shard = shard_of(turn)
             for when, todo in at.items():
                 @pl.when(step == when)
@@ -418,9 +419,9 @@
             if step > 1:
                 todo.append(functools.partial(gather.from_xy, k, step - 2))
         for step in range(max(zs - 2, 0), zs):
+            if last is not None and step == zs - 1:
+                todo.append(functools.partial(gather.own_out, last))
             todo.append(functools.partial(gather.from_xy, k, step))
-        if last is not None:
-            todo.append(functools.partial(gather.own_out, last))
         count = len(todo)
         return [(start + (stop - start) * i / max(count - 1, 1), e) for i, e in enumerate(todo)]
 
@@ -431,7 +432,7 @@
     half = CORES / shards
     sweep(
         0,
-        [(half, functools.partial(gather.from_diagonal, 0))] + relay(1, 0.1, 0.95, 2),
+        [(half, functools.partial(gather.from_diagonal, 0))] + relay(1, 0.06, 0.75, 2),
         attention_step,
     )
 
@@ -451,11 +452,19 @@
         hidden_step,
     )
 
+    together = 2 - points % 2
+
     def residual_step(shard, point):
-        product = times_transposed(hidden[shard, point], weights(2, shard))
-        tokens[point] += part(point, 5) * product
-
-    sweep(2, [(half, functools.partial(gather.from_diagonal, 2))], residual_step)
+        units = hidden[shard, pl.ds(point, together)]
+        count, token_count = units.shape[:2]
+        units = units.reshape(count * token_count, block_width)
+        product = times_transposed(units, weights(2, shard))
+        for i in range(count):
+            rows = product[i * token_count : (i + 1) * token_count]
+            tokens[point + i] += part(point + i, 5) * rows
+
+    last_events = [(half, functools.partial(gather.from_diagonal, 2))]
+    sweep(2, last_events, residual_step, together)
 
     def leave(point, carry):
         final_in = modulated(tokens[point], point, 6)

time: 189 us -> 187 us (0.989)
  Pallas kernels: 181 us -> 179 us
    pallas_call x1, Pallas kernels: 181 us -> 179 us  [denoise(): pl.pallas_call(functools.partial(denoise_kernel, sizes, HEADS // shards,...]
where the time goes in v3:
time: 187 us; the launch traced here: 186 us
  Pallas kernels  179 us (96%)
  other arithmetic  4.15 us (2%)
  local copies, waits for them, and re-layouts  2.79 us (1%)
    pallas_call x1, Pallas kernels, denoise(): pl.pallas_call(functools.partial(denoise_kernel, sizes, HEADS // shards,...  179 us

profile of v3, /device:TPU:0, one launch (start us, length us, event | category | flops | bytes accessed | tf_op | source)
XLA Modules:
  0.0 186.4 jit_solution(4643524279495138937)
XLA Ops:
  0.6 0.0 copy-start
  0.6 1.1 maximum_bitcast_fusion
  1.8 2.2 %pad_maximum_fusion.own_ref = bf16[3,144,1152]{2,1,0:T(8,128)(2,1)} fusion(bf16[1,144,1152]{2,1,0:T(8,128)(2,1)} %bitcast.8, bf16[1,144,1152]{2,1,0:T(8,128)(2,1)} %bitcast.9, bf16[1,144,1152]{2,1,0:T(8,128)(2,1)S(1)} %maximum_bitcast_fusion), kind=kLoop, calls=%fused_computation | loop fusion | flops 995328 | bytes 1990656 | tf_op jit(solution)/shard_map/stack | solution.py:586
  3.9 0.0 copy-done
  3.9 0.7 reshape.13.latent_ref
  4.6 178.8 %denoise.1 = (f32[2,16,4,128]{3,2,1,0:T(4,128)}, f32[2,16,4,128]{3,2,1,0:T(4,128)}) custom-call(s32[16]{0:T(128)} %shift_ref.1, s32[16]{0:T(128)} %start_ref.1, s32[16]{0:T(128)} %label_ref.1, f32[2,16,4,128]{3,2,1,0:T(4,128)} %reshape.13.latent_ref, f32[34,256]{1,0:T(8,128)} %constant.5.clone.table_ref, bf16[16,1152]{1,0:T(8,128)(2,1)} %w_patch_ref.1, ...), custom_call_target="tpu_custom_call" | custom-call | tf_op jit(solution)/shard_map/denoise/pallas_call | solution.py:528
  183.4 1.5 reshape.14
  184.9 0.9 convert_element_type.3
  185.8 0.6 reshape.15
Async XLA Ops:
  0.6 3.3 %copy-start = (f32[2,16,512]{2,1,0:T(8,128)S(1)}, f32[2,16,512]{2,1,0:T(8,128)}, u32[]{:S(2)}) copy-start(f32[2,16,512]{2,1,0:T(8,128)} %param.16) | copy-start | bytes 196612
